TPU v7x, 128 devices: a whole 4x4x4 slice. The times are simulated.
128 devices in a mesh: row: 16 (over x, y_lo, core), col: 8 (over y_hi, z).
Axes of the slice: x: 4, y: 4 (y_hi: 2, y_lo: 2; y = y_hi * 2 + y_lo), z: 4, core: 2. Of those that a mesh axis runs over, the one named last changes fastest.
Arguments:
- pair_in: bfloat16 [768, 768, 128], P('row', 'col'), may hold values from -6 to 6
- coords: float32 [3, 768], P(None, 'row'), may hold values from -36 to 36
- chain_ids: int32 [768], P('row'), may hold values from 0 to 3, never falling along the last dimension, each value on 1 to 384 neighbouring positions
- coord_mask: int32 [768], P('row'), may hold values 0 or 1
- gain_tri: float32 [128], replicated, may hold values from 0.1 to 1.9
- gain_sum: float32 [128], replicated, may hold values from 0.1 to 1.9
- gain_attn: float32 [128], replicated, may hold values from 0.1 to 1.9
- w_tri_in: bfloat16 [128, 640], replicated, may hold values from -0.5 to 0.5
- w_tri_out: bfloat16 [128, 128], replicated, may hold values from -0.5 to 0.5
- w_bins: float32 [36, 128], replicated, may hold values from -3 to 3
- same_chain: float32 [128], replicated, may hold values from -6 to 6
- w_query: bfloat16 [128, 128], replicated, may hold values from -8 to 8
- w_attn: bfloat16 [128, 384], replicated, may hold values from -0.5 to 0.5
- w_bias: bfloat16 [128, 4], replicated, may hold values from -0.5 to 0.5
- w_attn_out: bfloat16 [128, 128], replicated, may hold values from -0.5 to 0.5
Outputs:
- pair_out: bfloat16 [768, 768, 128], P('row', 'col')
Inputs may be any that keep to these rules, and one draw needn't show every extreme that they name: `chain_ids`: chain numbers never fall along the residues, and no chain holds more than half of them.
All inputs are finite; a program needn't handle non-finite values. No bound on the sum of `coord_mask` on one device may be relied on, other than what follows from the above.
Results may differ from a plain program's by a relative error of at most 0.02.
Values may be sent and summed in bfloat16 or wider, within the bound.
No kernel may reach another device: no remote copies, remote signals or barrier semaphores. Data moves between devices by JAX's collectives and lax.ppermute only.
A program may use at most 192 MiB of HBM per device.

v0:
```python
import math
import jax
import jax.numpy as jnp
from jax import lax
from jax.sharding import PartitionSpec as P


def joined_along(tiles, dim):
    lengths = list(tiles.shape[1:])
    lengths[dim] *= tiles.shape[0]
    return jnp.moveaxis(tiles, 0, dim).reshape(lengths)


def from_everyone(array, axis):
    copies = jnp.broadcast_to(array, (lax.axis_size(axis), *array.shape))
    return lax.all_to_all(copies, axis, split_axis=0, concat_axis=0, tiled=True)


def gather_directly(array, axis, dim):
    return joined_along(from_everyone(array, axis), dim)


def layer_norm(values, gain):
    center = values - jnp.mean(values, axis=-1, keepdims=True)
    spread = jnp.mean(center * center, axis=-1, keepdims=True)
    return center * lax.rsqrt(spread + 1e-05) * gain


def body(
    pair_in,
    coords,
    chain_ids,
    coord_mask,
    gain_tri,
    gain_sum,
    gain_attn,
    w_tri_in,
    w_tri_out,
    w_bins,
    same_chain,
    w_query,
    w_attn,
    w_bias,
    w_attn_out,
):
    n_rows = lax.axis_size("row")
    n_cols = lax.axis_size("col")
    row_count, col_count, channels = pair_in.shape
    n_heads = w_bias.shape[1]
    head_size = channels // n_heads
    n_bins = w_bins.shape[0]
    total_res = row_count * n_rows
    stride = col_count // n_rows
    col_start = lax.axis_index("col") * col_count
    coords_all, chains_all, masks_all = (
        gather_directly(coords, "row", 1),
        gather_directly(chain_ids, "row", 0),
        gather_directly(coord_mask, "row", 0),
    )
    pair_wide = pair_in.astype(jnp.float32)
    normed = layer_norm(pair_wide, gain_tri).astype(jnp.bfloat16)
    projected = jnp.dot(
        normed.reshape(row_count * col_count, channels),
        w_tri_in,
        preferred_element_type=jnp.float32,
    ).reshape(row_count, col_count, 5 * channels)
    left_side = (
        (jax.nn.sigmoid(projected[..., :channels]) * projected[..., channels : 2 * channels])
        .astype(jnp.bfloat16)
        .transpose(2, 0, 1)
    )
    right_side = (
        (
            jax.nn.sigmoid(projected[..., 2 * channels : 3 * channels])
            * projected[..., 3 * channels : 4 * channels]
        )
        .astype(jnp.bfloat16)
        .transpose(2, 0, 1)
    )
    tri_gate = jax.nn.sigmoid(projected[..., 4 * channels :])
    left_rows = lax.all_gather(left_side, "col", axis=2, tiled=True)
    left_perm = (
        left_rows.reshape(channels, row_count, n_cols, n_rows, stride)
        .transpose(0, 1, 3, 2, 4)
        .reshape(channels, row_count, total_res)
    )
    moved = lax.all_to_all(
        lax.all_to_all(right_side, "row", split_axis=2, concat_axis=1, tiled=True),
        "col",
        split_axis=1,
        concat_axis=2,
        tiled=True,
    )
    product = jnp.einsum(
        "cik,cjk->cij",
        left_perm,
        lax.all_gather(moved, "row", axis=2, tiled=True),
        preferred_element_type=jnp.float32,
    ).transpose(1, 2, 0)
    summed_norm = layer_norm(product, gain_sum).astype(jnp.bfloat16)
    pair_one = pair_wide + tri_gate * jnp.dot(
        summed_norm.reshape(row_count * col_count, channels),
        w_tri_out,
        preferred_element_type=jnp.float32,
    ).reshape(row_count, col_count, channels)
    far_coords = lax.dynamic_slice_in_dim(coords_all, col_start, col_count, 1)
    far_chains = lax.dynamic_slice_in_dim(chains_all, col_start, col_count, 0)
    far_masks = lax.dynamic_slice_in_dim(masks_all, col_start, col_count, 0)
    offsets = coords[:, :, None] - far_coords[:, None, :]
    dist = jnp.sqrt(jnp.sum(offsets * offsets, axis=0) + 1.0)
    centres = 2.0 + 20.0 * jnp.arange(n_bins, dtype=jnp.float32) / (n_bins - 1)
    spacing = 25.0 / (n_bins - 1)
    pair_mask = coord_mask.astype(jnp.float32)[:, None] * far_masks.astype(jnp.float32)[None, :]
    feats = jnp.exp(-(((dist[..., None] - centres) / spacing) ** 2)) * pair_mask[..., None]
    binned = jnp.dot(feats.reshape(row_count * col_count, n_bins), w_bins).reshape(
        row_count, col_count, channels
    )
    shared = (chain_ids[:, None] == far_chains[None, :]).astype(jnp.float32)
    pair_two = (pair_one + binned + shared[..., None] * same_chain).astype(jnp.bfloat16)
    normed_two = layer_norm(pair_two.astype(jnp.float32), gain_attn).astype(jnp.bfloat16)
    flat_two = normed_two.reshape(row_count * col_count, channels)
    queries = (
        jnp.dot(flat_two, w_query, preferred_element_type=jnp.float32)
        .astype(jnp.bfloat16)
        .reshape(row_count, col_count, n_heads, head_size)
    )
    gate_pre = jnp.dot(
        flat_two, w_attn[:, 2 * channels :], preferred_element_type=jnp.float32
    ).reshape(row_count, col_count, channels)
    attn_gate = jax.nn.sigmoid(gate_pre)
    pair_bias = (
        jnp.dot(flat_two, w_bias, preferred_element_type=jnp.float32)
        .astype(jnp.bfloat16)
        .reshape(row_count, col_count, n_heads)
        .transpose(2, 0, 1)
    )
    bias_moved = lax.all_to_all(
        lax.all_to_all(pair_bias, "row", split_axis=2, concat_axis=1, tiled=True),
        "col",
        split_axis=1,
        concat_axis=2,
        tiled=True,
    )
    bias_gathered = gather_directly(bias_moved, "row", 2)
    bias_mine = (
        bias_gathered.reshape(n_heads, col_count, n_rows, n_cols, stride)
        .transpose(0, 1, 3, 2, 4)
        .reshape(n_heads, col_count, total_res)
    )
    group = math.gcd(row_count, 8)
    blocks = row_count // group
    query_groups = queries.reshape(blocks, group, col_count, n_heads, head_size)
    root_dim = math.sqrt(head_size)
    start_state = (
        jnp.full((blocks, group, n_heads, col_count), -1e30, jnp.float32),
        jnp.zeros((blocks, group, n_heads, col_count), jnp.float32),
        jnp.zeros((blocks, group, n_heads, col_count, head_size), jnp.float32),
    )
    panel = lax.all_gather(normed_two, "col", axis=1, tiled=True)
    span = panel.shape[1]
    both = jnp.dot(
        panel.reshape(row_count * span, channels),
        w_attn[:, : 2 * channels],
        preferred_element_type=jnp.float32,
    ).reshape(row_count, span, 2 * channels)
    key_part = both[..., :channels].astype(jnp.bfloat16)
    span = key_part.shape[1]
    bias_part = bias_mine.astype(jnp.float32)
    key_groups = key_part.reshape(blocks, group, span, n_heads, head_size)
    value_groups = (
        both[..., channels:].astype(jnp.bfloat16).reshape(blocks, group, span, n_heads, head_size)
    )

    def one_block(items):
        query_blk, key_blk, value_blk, running_top, running_total, running_acc = items
        scores = (
            jnp.einsum("ijhd,ikhd->ihjk", query_blk, key_blk, preferred_element_type=jnp.float32)
            / root_dim
            + bias_part[None]
        )
        new_top = jnp.maximum(running_top, jnp.max(scores, axis=-1))
        rescale = jnp.exp(running_top - new_top)
        expo = jnp.exp(scores - new_top[..., None])
        new_total = running_total * rescale + jnp.sum(expo, axis=-1)
        new_acc = running_acc * rescale[..., None] + jnp.einsum(
            "ihjk,ikhd->ihjd",
            expo.astype(jnp.bfloat16),
            value_blk,
            preferred_element_type=jnp.float32,
        )
        return (new_top, new_total, new_acc)

    final_top, final_total, final_acc = lax.map(
        one_block,
        (query_groups, key_groups, value_groups, start_state[0], start_state[1], start_state[2]),
    )
    attended = (
        (final_acc / final_total[..., None])
        .reshape(row_count, n_heads, col_count, head_size)
        .transpose(0, 2, 1, 3)
        .reshape(row_count, col_count, channels)
    )
    gated = (attn_gate * attended).astype(jnp.bfloat16)
    result = pair_two.astype(jnp.float32) + jnp.dot(
        gated.reshape(row_count * col_count, channels),
        w_attn_out,
        preferred_element_type=jnp.float32,
    ).reshape(row_count, col_count, channels)
    return result.astype(jnp.bfloat16)


def solution(mesh):
    return jax.shard_map(
        body,
        mesh=mesh,
        in_specs=(
            P("row", "col", None),
            P(None, "row"),
            P("row"),
            P("row"),
            P(),
            P(),
            P(),
            P(),
            P(),
            P(),
            P(),
            P(),
            P(),
            P(),
            P(),
        ),
        out_specs=P("row", "col", None),
        check_vma=False,
    )
```

profile of v0, /device:TPU:0, one launch (start us, length us, event | category | flops | bytes accessed | tf_op | source)
XLA Modules:
  0.0 540.9 jit_solution(7241919329803855443)
XLA Ops:
  18.4 23.0 %all_to_all.94 = bf16[128,48,96]{0,1,2:T(8,128)(2,1)S(1)} all-to-all(bf16[128,48,96]{0,1,2:T(8,128)(2,1)S(1)} %copy.109), channel_id=1, replica_groups=mesh['row'=16,'col'=8] {'row'}, dimensions={2} | all-to-all | bytes 2359296 | tf_op jit(solution)/shard_map/all_to_all | solution.py:88
  42.3 35.2 %all_to_all.95 = bf16[128,768,6]{0,2,1:T(8,128)(2,1)S(1)} all-to-all(bf16[128,768,6]{0,2,1:T(8,128)(2,1)S(1)} %copy.111), channel_id=1, replica_groups=mesh['row'=16,'col'=8] {'col'}, dimensions={1} | all-to-all | bytes 2359296 | tf_op jit(solution)/shard_map/all_to_all | solution.py:87
  79.5 9.9 %all_to_all.96 = s32[16,1,48]{2,1,0:T(1,128)S(1)} all-to-all(s32[16,1,48]{2,1,0:T(1,128)S(1)} %broadcast_in_dim.13), channel_id=1, replica_groups=mesh['row'=16,'col'=8] {'row'}, dimensions={0} | all-to-all | bytes 6144 | tf_op jit(solution)/shard_map/all_to_all | solution.py:16
  104.4 4.6 all-to-all-done.2
  110.7 48.2 %all-gather.4.cloned.1.call-done = bf16[128,48,768]{0,2,1:T(8,128)(2,1)} async-done(((bf16[128,48,96]{0,2,1:T(8,128)(2,1)}), bf16[128,48,768]{0,2,1:T(8,128)(2,1)}) %all-gather.4.cloned.1.call-update) | async-done | bytes 9437200 | tf_op jit(solution)/shard_map/all_gather | solution.py:81
  158.9 13.4 %copy.107 = bf16[128,48,768]{0,1,2:T(8,128)(2,1)} copy(bf16[128,48,768]{0,2,1:T(8,128)(2,1)} %all-gather.4.cloned.1.call-done) | data formatting | bytes 18874368 | tf_op jit(solution)/shard_map/all_gather | solution.py:81
  172.2 10.0 %copy.108 = bf16[128,48,16,8,6]{0,1,4,3,2:T(8,128)(2,1)} copy(bf16[128,48,16,8,6]{0,1,4,2,3:T(8,128)(2,1)} %bitcast.128) | data formatting | bytes 18874368 | tf_op jit(solution)/shard_map/transpose | solution.py:84
  182.2 14.3 %copy.115 = bf16[128,48,768]{2,1,0:T(8,128)(2,1)} copy(bf16[128,48,768]{0,1,2:T(8,128)(2,1)} %bitcast.129) | data formatting | bytes 18874368 | tf_op jit(solution)/shard_map/reshape | solution.py:85
  196.6 92.8 %all-gather.6.cloned.1.call-done = bf16[128,96,768]{1,2,0:T(8,128)(2,1)} async-done(((bf16[128,96,48]{1,2,0:T(8,128)(2,1)}), bf16[128,96,768]{1,2,0:T(8,128)(2,1)}) %all-gather.6.cloned.1.call-update) | async-done | bytes 18874384 | tf_op jit(solution)/shard_map/all_gather | solution.py:97
  289.3 13.4 %bitcast_reduce_fusion = (f32[48,96]{1,0:T(8,128)S(1)}, f32[128,48,96]{2,1,0:T(8,128)S(1)}) fusion(bf16[128,48,768]{2,1,0:T(8,128)(2,1)} %copy.115, bf16[128,96,768]{1,2,0:T(8,128)(2,1)} %all-gather.6.cloned.1.call-done), kind=kOutput, calls=%fused_computation.32 | convolution fusion | flops 906554880 | bytes 30689280 | tf_op jit(solution)/shard_map/cik,cjk->cij/dot_general | solution.py:94
  315.5 10.9 %all_to_all.97 = bf16[16,2,576]{2,1,0:T(2,128)(2,1)S(1)} all-to-all(bf16[16,2,576]{2,1,0:T(2,128)(2,1)S(1)} %reshape.272), channel_id=1, replica_groups=mesh['row'=16,'col'=8] {'row'}, dimensions={0} | all-to-all | bytes 73728 | tf_op jit(solution)/shard_map/all_to_all | solution.py:138
  328.5 14.5 %all_to_all.98 = bf16[8,2,1152]{2,1,0:T(2,128)(2,1)S(1)} all-to-all(bf16[8,2,1152]{2,1,0:T(2,128)(2,1)S(1)} %reshape.274), channel_id=1, replica_groups=mesh['row'=16,'col'=8] {'col'}, dimensions={0} | all-to-all | bytes 73728 | tf_op jit(solution)/shard_map/all_to_all | solution.py:137
  353.8 10.0 %all-to-all-done.7 = bf16[16,4,96,48]{2,3,1,0:T(8,128)(2,1)S(1)} async-done(((bf16[16,4,96,48]{2,3,1,0:T(8,128)(2,1)}), bf16[16,4,96,48]{2,3,1,0:T(8,128)(2,1)S(1)}, u32[]{:S(2)}, u32[]{:S(2)}) %all-to-all-start.7) | async-done | bytes 589856 | tf_op jit(solution)/shard_map/all_to_all | solution.py:16
  365.9 64.9 %all-gather.8.cloned.1.call-done = bf16[48,768,128]{2,1,0:T(8,128)(2,1)} async-done(((bf16[48,96,128]{2,1,0:T(8,128)(2,1)}), bf16[48,768,128]{2,1,0:T(8,128)(2,1)}) %all-gather.8.cloned.1.call-update) | async-done | bytes 9437200 | tf_op jit(solution)/shard_map/all_gather | solution.py:159
  430.8 11.4 %convolution_convert_fusion = bf16[48,768,256]{1,2,0:T(8,128)(2,1)} fusion(bf16[48,768,128]{2,1,0:T(8,128)(2,1)} %all-gather.8.cloned.1.call-done, bf16[128,384]{1,0:T(8,128)(2,1)S(1)} %copy-done.7), kind=kOutput, calls=%fused_computation.22 | convolution fusion | flops 2425356288 | bytes 28377088 | tf_op jit(solution)/shard_map/dot_general | solution.py:161
  442.3 14.3 %fusion.89 = (bf16[48,768,128]{1,2,0:T(8,128)(2,1)}, bf16[48,768,128]{1,2,0:T(8,128)(2,1)}) fusion(bf16[48,768,256]{1,2,0:T(8,128)(2,1)} %convolution_convert_fusion), kind=kLoop, calls=%fused_computation.111 | loop fusion | bytes 37748736 | tf_op jit(solution)/shard_map/slice | solution.py:171
  456.6 68.5 %while.12 = (s32[]{:T(128)}, f32[6,8,4,96]{3,2,1,0:T(4,128)S(1)}, f32[6,8,4,96,32]{3,4,2,1,0:T(8,128)}, bf16[6,8,96,4,32]{2,1,0,4,3:T(8,128)(2,1)}, bf16[6,8,768...) while((s32[]{:T(128)}, f32[6,8,4,96]{3,2,1,0:T(4,128)S(1)}, ...), condition=%wide.region_10.11_spmd, body=%wide.region_7.10_spmd.sunk | while | flops 328055808 | bytes 36259420 | solution.py:193
  460.6 5.0 fusion.110
  472.0 5.0 fusion.110
  483.4 5.0 fusion.110
  494.9 4.9 fusion.110
  506.3 5.0 fusion.110
  517.7 4.9 fusion.110
  529.7 4.4 fusion.41
  (145 shorter events, 102.1 us)
Async XLA Ops:
  6.5 4.6 copy-start
  6.5 4.6 copy-start.4
  6.5 4.6 copy-start.13
  6.5 152.3 %all-gather.4.cloned.1.call-start = ((), (), s32[]{:S(2)}) async-start(), calls=%async_computation.8 | async-start | bytes 10616832 | tf_op jit(solution)/shard_map/all_gather | solution.py:81
  13.2 4.7 copy-start.2
  17.9 271.4 %all-gather.6.cloned.1.call-start = ((), (), s32[]{:S(2)}) async-start(), calls=%async_computation.9 | async-start | bytes 26738688 | tf_op jit(solution)/shard_map/all_gather | solution.py:97
  77.7 1.8 copy-start.15
  77.7 11.7 %copy-start.11 = (s32[48]{0:T(128)S(1)}, s32[48]{0:T(128)}, u32[]{:S(2)}) copy-start(s32[48]{0:T(128)} %param.19) | copy-start | bytes 580
  77.7 15.8 %copy-start.10 = (f32[3,48]{1,0:T(4,128)S(1)}, f32[3,48]{1,0:T(4,128)}, u32[]{:S(2)}) copy-start(f32[3,48]{1,0:T(4,128)} %param.18) | copy-start | bytes 1732
  90.0 9.4 %all-to-all-start.4 = ((s32[16,1,48]{2,1,0:T(1,128)}), s32[16,1,48]{2,1,0:T(1,128)S(1)}, u32[]{:S(2)}, u32[]{:S(2)}) async-start(s32[16,1,48]{2,1,0:T(1,128)} %broadcast_in_dim.14), calls=%async_computation.4 | async-start | bytes 16384 | tf_op jit(solution)/shard_map/all_to_all | solution.py:16
  99.4 9.5 %all-to-all-start.2 = ((f32[16,1,144]{2,1,0:T(1,128)}), f32[16,1,144]{2,1,0:T(1,128)S(1)}, u32[]{:S(2)}, u32[]{:S(2)}) async-start(f32[16,1,144]{2,1,0:T(1,128)} %reshape.270), calls=%async_computation.2 | async-start | bytes 32768 | tf_op jit(solution)/shard_map/all_to_all | solution.py:16
  102.9 327.9 %all-gather.8.cloned.1.call-start = ((), (), s32[]{:S(2)}) async-start(), calls=%async_computation.10 | async-start | bytes 10616832 | tf_op jit(solution)/shard_map/all_gather | solution.py:159
  304.1 1.3 copy-start.5
  304.1 1.3 copy-start.18
  304.1 1.3 copy-start.19
  305.4 5.5 %copy-start.16 = (f32[128]{0:T(128)S(1)}, f32[128]{0:T(128)}, u32[]{:S(2)}) copy-start(f32[128]{0:T(128)} %param.23) | copy-start | bytes 1540
  309.2 1.7 copy-start.6
  309.2 4.2 copy-start.12
  327.3 22.9 %copy-start.3 = (bf16[48,96,128]{2,1,0:T(8,128)(2,1)S(1)}, bf16[48,96,128]{2,1,0:T(8,128)(2,1)}, u32[]{:S(2)}) copy-start(bf16[48,96,128]{2,1,0:T(8,128)(2,1)} %fusion.34) | copy-start | bytes 3538948
  327.3 22.9 %copy-start.9 = (bf16[128,128]{1,0:T(8,128)(2,1)S(1)}, bf16[128,128]{1,0:T(8,128)(2,1)}, u32[]{:S(2)}) copy-start(bf16[128,128]{1,0:T(8,128)(2,1)} %param.28) | copy-start | bytes 98308
  346.3 17.4 %all-to-all-start.7 = ((bf16[16,4,96,48]{2,3,1,0:T(8,128)(2,1)}), bf16[16,4,96,48]{2,3,1,0:T(8,128)(2,1)S(1)}, u32[]{:S(2)}, u32[]{:S(2)}) async-start(bf16[16,4,96,48]{2,3,1,0:T(8,128)(2,1)} %broadcast_in_dim.15), calls=%async_computation.7 | async-start | bytes 1572864 | tf_op jit(solution)/shard_map/all_to_all | solution.py:16
  364.2 66.6 %copy-start.7 = (bf16[128,384]{1,0:T(8,128)(2,1)S(1)}, bf16[128,384]{1,0:T(8,128)(2,1)}, u32[]{:S(2)}) copy-start(bf16[128,384]{1,0:T(8,128)(2,1)} %param.29) | copy-start | bytes 294916
  527.5 2.2 copy-start.17
  529.7 4.4 copy-start.1
  (2 other events, 1.4 us)
Sparse Core Ops, SparseCore 0:
  18.0 140.8 all-gather.3
  160.5 128.7 all-gather.5
  313.5 117.2 all-gather.7
where the time goes:
time: 548 us; the launch traced here: 541 us
  waiting for transfers between devices  224 us (41%)
  blocking collectives  93.4 us (17%)
  matrix products  85.5 us (16%)
  local copies, waits for them, and re-layouts  79.8 us (15%)
  other arithmetic  32.5 us (6%)
  between operations  13.9 us (3%)
  starting transfers between devices  11.3 us (2%)
    all_gather x1, waiting for transfers between devices, body(): lax.all_gather(moved, 'row', axis=2, tiled=True)  92.8 us
    all_gather x1, waiting for transfers between devices, body(): panel = lax.all_gather(normed_two, 'col', axis=1, tiled=True)  64.9 us
    all_gather x1, waiting for transfers between devices, body(): left_rows = lax.all_gather(left_side, 'col', axis=2, tiled=True)  48.2 us
    all_to_all x1, blocking collectives, body(): lax.all_to_all(lax.all_to_all(right_side, 'row', split_axis=2, concat_axi...  35.2 us
    dot_general x6, matrix products, one_block(): jnp.einsum('ihjk,ikhd->ihjd', expo.astype(jnp.bfloat16), value_blk, prefe...  29.8 us
    all_to_all x1, blocking collectives, body(): lax.all_to_all(right_side, 'row', split_axis=2, concat_axis=1, tiled=True)  23 us
    all_to_all x3, waiting for transfers between devices, from_everyone(): return lax.all_to_all(copies, axis, split_axis=0, concat_axis=0, tiled=True)  18.5 us
    dot_general x6, matrix products, one_block(): jnp.einsum('ijhd,ikhd->ihjk', query_blk, key_blk, preferred_element_type=...  17.9 us
  transfers between devices with their start and end apart: 6, of which 6 were waited for; matrix products, arithmetic and copies ran while one was open for 11% of the time, Pallas kernels for 0%

commit v1 on v0

--- a/solution.py
+++ b/solution.py
@@ -78,7 +78,9 @@
         .transpose(2, 0, 1)
     )
     tri_gate = jax.nn.sigmoid(projected[..., 4 * channels :])
-    left_rows = lax.all_gather(left_side, "col", axis=2, tiled=True)
+    left_rows = jnp.concatenate(
+        lax.all_to_all(jnp.stack([left_side] * lax.axis_size("col")), "col", 0, 0), axis=2
+    )
     left_perm = (
         left_rows.reshape(channels, row_count, n_cols, n_rows, stride)
         .transpose(0, 1, 3, 2, 4)

time: 548 us -> 618 us (1.13)
  waiting for transfers between devices: 224 us -> 266 us
  local copies, waits for them, and re-layouts: 79.8 us -> 105 us
    all_to_all x0 -> x1, waiting for transfers between devices: none -> 185 us  [body(): lax.all_to_all(jnp.stack([left_side] * lax.axis_size('col')), 'col', 0, 0)]
    all_gather x1, waiting for transfers between devices: 92.8 us -> 0.01 us  [body(): lax.all_gather(moved, 'row', axis=2, tiled=True)]
    all_gather x1 -> x0, waiting for transfers between devices: 48.2 us -> none  [body(): left_rows = lax.all_gather(left_side, 'col', axis=2, tiled=True)]
    all_to_all x0 -> x1, local copies, waits for them, and re-layouts: none -> 18.2 us  [body(): lax.all_to_all(jnp.stack([left_side] * lax.axis_size('col')), 'col', 0, 0)]
    transpose x1, local copies, waits for them, and re-layouts: 9.99 us -> 25.2 us  [body(): left_perm = left_rows.reshape(channels, row_count, n_cols, n_rows, stride...]
    all_gather x1 -> x0, local copies, waits for them, and re-layouts: 13.4 us -> none  [body(): left_rows = lax.all_gather(left_side, 'col', axis=2, tiled=True)]
    all_to_all x1 -> x2, blocking collectives: 9.89 us -> 17.4 us  [from_everyone(): return lax.all_to_all(copies, axis, split_axis=0, concat_axis=0, tiled=True)]
    all_to_all x3 -> x2, waiting for transfers between devices: 18.5 us -> 16 us  [from_everyone(): return lax.all_to_all(copies, axis, split_axis=0, concat_axis=0, tiled=True)]
  transfers between devices with their start and end apart: 6 -> 5, of which waited for: 6 -> 4; matrix products, arithmetic and copies ran while one was open for 11% -> 13% of each run, Pallas kernels for 0% -> 0%
where the time goes in v1:
time: 618 us; the launch traced here: 610 us
  waiting for transfers between devices  266 us (43%)
  local copies, waits for them, and re-layouts  105 us (17%)
  blocking collectives  94.7 us (15%)
  matrix products  85.4 us (14%)
  other arithmetic  30.9 us (5%)
  between operations  14.3 us (2%)
  starting transfers between devices  12.7 us (2%)
    all_to_all x1, waiting for transfers between devices, body(): lax.all_to_all(jnp.stack([left_side] * lax.axis_size('col')), 'col', 0, 0)  185 us
    all_gather x1, waiting for transfers between devices, body(): panel = lax.all_gather(normed_two, 'col', axis=1, tiled=True)  64.9 us
    all_to_all x1, blocking collectives, body(): lax.all_to_all(lax.all_to_all(right_side, 'row', split_axis=2, concat_axi...  30.5 us
    dot_general x6, matrix products, one_block(): jnp.einsum('ihjk,ikhd->ihjd', expo.astype(jnp.bfloat16), value_blk, prefe...  29.8 us
    transpose x1, local copies, waits for them, and re-layouts, body(): left_perm = left_rows.reshape(channels, row_count, n_cols, n_rows, stride...  25.2 us
    all_to_all x1, blocking collectives, body(): lax.all_to_all(right_side, 'row', split_axis=2, concat_axis=1, tiled=True)  22.9 us
    all_to_all x1, local copies, waits for them, and re-layouts, body(): lax.all_to_all(jnp.stack([left_side] * lax.axis_size('col')), 'col', 0, 0)  18.2 us
    dot_general x6, matrix products, one_block(): jnp.einsum('ijhd,ikhd->ihjk', query_blk, key_blk, preferred_element_type=...  17.9 us
  transfers between devices with their start and end apart: 5, of which 4 were waited for; matrix products, arithmetic and copies ran while one was open for 13% of the time, Pallas kernels for 0%

profile of v1, /device:TPU:0, one launch (start us, length us, event | category | flops | bytes accessed | tf_op | source)
XLA Modules:
  0.0 609.9 jit_solution(1166910758803442428)
XLA Ops:
  18.0 22.9 %all_to_all.99 = bf16[128,48,96]{0,1,2:T(8,128)(2,1)S(1)} all-to-all(bf16[128,48,96]{0,1,2:T(8,128)(2,1)S(1)} %copy.108), channel_id=1, replica_groups=mesh['row'=16,'col'=8] {'row'}, dimensions={2} | all-to-all | bytes 2359296 | tf_op jit(solution)/shard_map/all_to_all | solution.py:90
  41.8 30.5 %all_to_all.100 = bf16[128,768,6]{0,2,1:T(8,128)(2,1)S(1)} all-to-all(bf16[128,768,6]{0,2,1:T(8,128)(2,1)S(1)} %copy.110), channel_id=1, replica_groups=mesh['row'=16,'col'=8] {'col'}, dimensions={1} | all-to-all | bytes 2359296 | tf_op jit(solution)/shard_map/all_to_all | solution.py:89
  74.4 8.6 %all_to_all.101 = s32[16,1,48]{2,1,0:T(1,128)S(1)} all-to-all(s32[16,1,48]{2,1,0:T(1,128)S(1)} %broadcast_in_dim.13), channel_id=1, replica_groups=mesh['row'=16,'col'=8] {'row'}, dimensions={0} | all-to-all | bytes 6144 | tf_op jit(solution)/shard_map/all_to_all | solution.py:16
  87.3 6.0 all-to-all-done.5
  93.2 8.8 %all_to_all.102 = f32[16,1,144]{2,1,0:T(1,128)S(1)} all-to-all(f32[16,1,144]{2,1,0:T(1,128)S(1)} %reshape.272), channel_id=1, replica_groups=mesh['row'=16,'col'=8] {'row'}, dimensions={0} | all-to-all | bytes 18432 | tf_op jit(solution)/shard_map/all_to_all | solution.py:16
  102.0 5.2 stack.2
  107.3 5.1 all-to-all-start
  116.6 185.4 %all-to-all-done = bf16[8,128,48,96]{1,3,2,0:T(8,128)(2,1)} async-done(((bf16[8,128,48,96]{1,3,2,0:T(8,128)(2,1)}), bf16[8,128,48,96]{1,3,2,0:T(8,128)(2,1)}, u32[]{:S(2)}, u32[]{:S(2)}) %all-to-all-start) | async-done | bytes 9437216 | tf_op jit(solution)/shard_map/all_to_all | solution.py:82
  302.1 18.2 %copy.106 = bf16[8,128,48,96]{1,0,3,2:T(8,128)(2,1)} copy(bf16[8,128,48,96]{1,3,2,0:T(8,128)(2,1)} %all-to-all-done) | data formatting | bytes 18874368 | tf_op jit(solution)/shard_map/all_to_all | solution.py:82
  320.3 25.2 %copy.107 = bf16[128,48,16,8,6]{0,1,4,3,2:T(8,128)(2,1)} copy(bf16[128,48,16,8,6]{0,3,4,2,1:T(8,128)(2,1)} %bitcast.130) | data formatting | bytes 18874368 | tf_op jit(solution)/shard_map/transpose | solution.py:86
  345.5 14.0 %copy.114 = bf16[128,48,768]{2,1,0:T(8,128)(2,1)} copy(bf16[128,48,768]{0,1,2:T(8,128)(2,1)} %bitcast.131) | data formatting | bytes 18874368 | tf_op jit(solution)/shard_map/reshape | solution.py:87
  359.5 13.4 %bitcast_reduce_fusion = (f32[48,96]{1,0:T(8,128)S(1)}, f32[128,48,96]{2,1,0:T(8,128)S(1)}) fusion(bf16[128,48,768]{2,1,0:T(8,128)(2,1)} %copy.114, bf16[128,96,768]{1,2,0:T(8,128)(2,1)} %all-gather.3.cloned.1.call-done), kind=kOutput, calls=%fused_computation.32 | convolution fusion | flops 906554880 | bytes 30689280 | tf_op jit(solution)/shard_map/cik,cjk->cij/dot_general | solution.py:96
  385.7 10.0 %all_to_all.103 = bf16[16,2,576]{2,1,0:T(2,128)(2,1)S(1)} all-to-all(bf16[16,2,576]{2,1,0:T(2,128)(2,1)S(1)} %reshape.274), channel_id=1, replica_groups=mesh['row'=16,'col'=8] {'row'}, dimensions={0} | all-to-all | bytes 73728 | tf_op jit(solution)/shard_map/all_to_all | solution.py:140
  397.8 13.8 %all_to_all.104 = bf16[8,2,1152]{2,1,0:T(2,128)(2,1)S(1)} all-to-all(bf16[8,2,1152]{2,1,0:T(2,128)(2,1)S(1)} %reshape.276), channel_id=1, replica_groups=mesh['row'=16,'col'=8] {'col'}, dimensions={0} | all-to-all | bytes 73728 | tf_op jit(solution)/shard_map/all_to_all | solution.py:139
  422.3 10.0 %all-to-all-done.8 = bf16[16,4,96,48]{2,3,1,0:T(8,128)(2,1)S(1)} async-done(((bf16[16,4,96,48]{2,3,1,0:T(8,128)(2,1)}), bf16[16,4,96,48]{2,3,1,0:T(8,128)(2,1)S(1)}, u32[]{:S(2)}, u32[]{:S(2)}) %all-to-all-start.8) | async-done | bytes 589856 | tf_op jit(solution)/shard_map/all_to_all | solution.py:16
  434.5 64.9 %all-gather.5.cloned.1.call-done = bf16[48,768,128]{2,1,0:T(8,128)(2,1)} async-done(((bf16[48,96,128]{2,1,0:T(8,128)(2,1)}), bf16[48,768,128]{2,1,0:T(8,128)(2,1)}) %all-gather.5.cloned.1.call-update) | async-done | bytes 9437200 | tf_op jit(solution)/shard_map/all_gather | solution.py:161
  499.4 11.4 %convolution_convert_fusion = bf16[48,768,256]{1,2,0:T(8,128)(2,1)} fusion(bf16[48,768,128]{2,1,0:T(8,128)(2,1)} %all-gather.5.cloned.1.call-done, bf16[128,384]{1,0:T(8,128)(2,1)S(1)} %copy-done.7), kind=kOutput, calls=%fused_computation.22 | convolution fusion | flops 2425356288 | bytes 28377088 | tf_op jit(solution)/shard_map/dot_general | solution.py:163
  510.8 14.3 %fusion.89 = (bf16[48,768,128]{1,2,0:T(8,128)(2,1)}, bf16[48,768,128]{1,2,0:T(8,128)(2,1)}) fusion(bf16[48,768,256]{1,2,0:T(8,128)(2,1)} %convolution_convert_fusion), kind=kLoop, calls=%fused_computation.111 | loop fusion | bytes 37748736 | tf_op jit(solution)/shard_map/slice | solution.py:173
  525.1 68.5 %while.12 = (s32[]{:T(128)}, f32[6,8,4,96]{3,2,1,0:T(4,128)S(1)}, f32[6,8,4,96,32]{3,4,2,1,0:T(8,128)}, bf16[6,8,96,4,32]{2,1,0,4,3:T(8,128)(2,1)}, bf16[6,8,768...) while((s32[]{:T(128)}, f32[6,8,4,96]{3,2,1,0:T(4,128)S(1)}, ...), condition=%wide.region_10.11_spmd, body=%wide.region_7.10_spmd.sunk | while | flops 328055808 | bytes 36259420 | solution.py:195
  529.1 5.0 fusion.110
  540.5 5.0 fusion.110
  563.4 5.0 fusion.110
  574.8 5.0 fusion.110
  586.2 5.0 fusion.110
  (144 shorter events, 102.7 us)
Async XLA Ops:
  6.5 4.6 copy-start
  6.5 4.6 copy-start.4
  6.5 4.6 copy-start.13
  6.5 352.9 %all-gather.3.cloned.1.call-start = ((), (), s32[]{:S(2)}) async-start(), calls=%async_computation.9 | async-start | bytes 26738688 | tf_op jit(solution)/shard_map/all_gather | solution.py:99
  13.2 4.3 copy-start.2
  72.6 1.8 copy-start.15
  72.6 10.5 %copy-start.11 = (s32[48]{0:T(128)S(1)}, s32[48]{0:T(128)}, u32[]{:S(2)}) copy-start(s32[48]{0:T(128)} %param.19) | copy-start | bytes 580
  72.6 14.6 %copy-start.10 = (f32[3,48]{1,0:T(4,128)S(1)}, f32[3,48]{1,0:T(4,128)}, u32[]{:S(2)}) copy-start(f32[3,48]{1,0:T(4,128)} %param.18) | copy-start | bytes 1732
  83.7 9.6 %all-to-all-start.5 = ((s32[16,1,48]{2,1,0:T(1,128)}), s32[16,1,48]{2,1,0:T(1,128)S(1)}, u32[]{:S(2)}, u32[]{:S(2)}) async-start(s32[16,1,48]{2,1,0:T(1,128)} %broadcast_in_dim.14), calls=%async_computation.5 | async-start | bytes 16384 | tf_op jit(solution)/shard_map/all_to_all | solution.py:16
  107.3 194.8 %all-to-all-start = ((bf16[8,128,48,96]{1,3,2,0:T(8,128)(2,1)}), bf16[8,128,48,96]{1,3,2,0:T(8,128)(2,1)}, u32[]{:S(2)}, u32[]{:S(2)}) async-start(bf16[8,128,48,96]{1,3,2,0:T(8,128)(2,1)} %stack.2), calls=%async_computation | async-start | bytes 18874368 | tf_op jit(solution)/shard_map/all_to_all | solution.py:82
  112.4 387.0 %all-gather.5.cloned.1.call-start = ((), (), s32[]{:S(2)}) async-start(), calls=%async_computation.10 | async-start | bytes 10616832 | tf_op jit(solution)/shard_map/all_gather | solution.py:161
  373.5 0.8 copy-start.8
  374.3 1.3 copy-start.5
  374.3 1.3 copy-start.18
  374.3 1.3 copy-start.19
  375.5 5.5 copy-start.16
  379.3 1.7 copy-start.6
  379.3 4.2 copy-start.12
  396.6 22.2 %copy-start.3 = (bf16[48,96,128]{2,1,0:T(8,128)(2,1)S(1)}, bf16[48,96,128]{2,1,0:T(8,128)(2,1)}, u32[]{:S(2)}) copy-start(bf16[48,96,128]{2,1,0:T(8,128)(2,1)} %fusion.34) | copy-start | bytes 3538948
  396.6 22.2 %copy-start.9 = (bf16[128,128]{1,0:T(8,128)(2,1)S(1)}, bf16[128,128]{1,0:T(8,128)(2,1)}, u32[]{:S(2)}) copy-start(bf16[128,128]{1,0:T(8,128)(2,1)} %param.28) | copy-start | bytes 98308
  414.9 17.4 %all-to-all-start.8 = ((bf16[16,4,96,48]{2,3,1,0:T(8,128)(2,1)}), bf16[16,4,96,48]{2,3,1,0:T(8,128)(2,1)S(1)}, u32[]{:S(2)}, u32[]{:S(2)}) async-start(bf16[16,4,96,48]{2,3,1,0:T(8,128)(2,1)} %broadcast_in_dim.15), calls=%async_computation.8 | async-start | bytes 1572864 | tf_op jit(solution)/shard_map/all_to_all | solution.py:16
  432.8 66.6 %copy-start.7 = (bf16[128,384]{1,0:T(8,128)(2,1)S(1)}, bf16[128,384]{1,0:T(8,128)(2,1)}, u32[]{:S(2)}) copy-start(bf16[128,384]{1,0:T(8,128)(2,1)} %param.29) | copy-start | bytes 294916
  596.1 2.2 copy-start.17
  598.3 4.4 copy-start.1
  (1 other events, 0.7 us)
Sparse Core Ops, SparseCore 0:
  74.5 212.1 all-gather.2
  383.7 115.6 all-gather.4
